TPU v7x, 32 devices: a whole 2x2x4 slice. The times are simulated.
32 devices in a mesh: ta: 8 (over y, x, core), gz: 4 (over z).
Axes of the slice: x: 2, y: 2, z: 4, core: 2. Of those that a mesh axis runs over, the one named last changes fastest.
Arguments:
- source: bfloat16 [8, 4, 2, 4, 3, 12, 256], P('ta', 'gz'), may hold values from -6 to 6
- gauge_field: bfloat16 [8, 4, 4, 2, 3, 3, 256], P('ta', 'gz'), may hold values from -2.5 to 2.5
Outputs:
- twice_applied: bfloat16 [8, 4, 2, 4, 3, 12, 256], P('ta', 'gz')
All inputs are finite; a program needn't handle non-finite values.
Results may differ from a plain program's by a relative error of at most 0.0075.
Values may be sent and summed in bfloat16 or wider, within the bound.
A program may use at most 64 MiB of HBM per device.

v0:
```python
import functools

import jax
import jax.numpy as jnp
from jax import lax
from jax.experimental import pallas as pl
from jax.experimental.pallas import tpu as pltpu
from jax.sharding import PartitionSpec as P

NX = 16
HOPPING = 0.124
GAMMA_PERM = ((3, 2, 1, 0), (3, 2, 1, 0), (2, 3, 0, 1), (2, 3, 0, 1))
GAMMA_PHASE = (
    ((0, 1), (0, 1), (0, -1), (0, -1)),
    ((-1, 0), (1, 0), (1, 0), (-1, 0)),
    ((0, 1), (0, -1), (0, -1), (0, 1)),
    ((1, 0), (1, 0), (1, 0), (1, 0)),
)
LANES = 128
MESH = pl.DeviceIdType.MESH

HALOS = ((3, 1), (3, -1), (2, 1), (2, -1))


def signed_sum(base, term, sign):
    if not isinstance(sign, int):
        return base + term * sign
    return base + term if sign > 0 else base - term


def rounded(first, second):
    return jnp.concatenate([first, second], 0).astype(jnp.bfloat16)


def project(psi, direction, hop_sign):
    out = []
    for s in range(2):
        partner = GAMMA_PERM[direction][s]
        pr, pi = GAMMA_PHASE[direction][s]
        row = []
        for c in range(3):
            if pi == 0:
                re = signed_sum(psi(0, s, c), psi(0, partner, c), -hop_sign * pr)
                im = signed_sum(psi(1, s, c), psi(1, partner, c), -hop_sign * pr)
            else:
                re = signed_sum(psi(0, s, c), psi(1, partner, c), hop_sign * pi)
                im = signed_sum(psi(1, s, c), psi(0, partner, c), -hop_sign * pi)
            row.append(rounded(re, im))
        out.append(row)
    return out


def widened(pair):
    wide = pair.astype(jnp.float32)
    return wide[:8], wide[8:]


def shift_sites(tile, direction, steps):
    lane = lax.broadcasted_iota(jnp.int32, (8, LANES), 1)
    if direction == 0:
        column = lane % NX
        if steps > 0:
            return jnp.where(
                column == NX - 1,
                pltpu.roll(tile, NX - 1, axis=1),
                pltpu.roll(tile, LANES - 1, axis=1),
            )
        return jnp.where(
            column == 0,
            pltpu.roll(tile, LANES - (NX - 1), axis=1),
            pltpu.roll(tile, 1, axis=1),
        )
    near = pltpu.roll(tile, LANES - NX if steps > 0 else NX, axis=1)
    first_half = lax.broadcasted_iota(jnp.int32, (8, LANES), 0) % 2 == 0
    other = jnp.where(first_half, pltpu.roll(near, 7, axis=0), pltpu.roll(near, 1, axis=0))
    return jnp.where(lane >= LANES - NX if steps > 0 else lane < NX, other, near)


def add_hop(acc, half, link, direction, hop_sign):
    for r in range(3):
        lr = [link(0, r, c) for c in range(3)]
        li = [link(1, r, c) for c in range(3)]
        k = []
        for s in range(2):
            re = im = None
            for c in range(3):
                hr, hi = half[s][c]
                tr = lr[c] * hr - li[c] * hi
                ti = lr[c] * hi + li[c] * hr
                re = tr if re is None else re + tr
                im = ti if im is None else im + ti
            k.append((re, im))
            acc[0][s][r] = acc[0][s][r] + re
            acc[1][s][r] = acc[1][s][r] + im
        for s in (2, 3):
            kr, ki = k[GAMMA_PERM[direction][s]]
            pr, pi = GAMMA_PHASE[direction][s]
            if pi == 0:
                acc[0][s][r] = signed_sum(acc[0][s][r], kr, -hop_sign * pr)
                acc[1][s][r] = signed_sum(acc[1][s][r], ki, -hop_sign * pr)
            else:
                acc[0][s][r] = signed_sum(acc[0][s][r], ki, hop_sign * pi)
                acc[1][s][r] = signed_sum(acc[1][s][r], kr, -hop_sign * pi)


def plane(ri, s, c):
    return (ri * 4 + s) * 3 + c


def link_slot(direction, hop_sign):
    return direction * 2 + (0 if hop_sign > 0 else 1)


def kernel(
    groups, source_hbm, gauge_hbm, out, source, gauge, wide, psi, acc, links, sent, got,
    links_below, load_sem, send_sem, recv_sem, link_send, link_recv,
):
    ta, gz = lax.axis_index("ta"), lax.axis_index("gz")
    nt, nz = lax.axis_size("ta"), lax.axis_size("gz")
    above_t = (lax.rem(ta + 1, nt), gz)
    below_t = (lax.rem(ta + nt - 1, nt), gz)
    above_z = (ta, lax.rem(gz + 1, nz))
    below_z = (ta, lax.rem(gz + nz - 1, nz))
    targets = (below_t, above_t, below_z, above_z)

    source_load = pltpu.make_async_copy(source_hbm, source, load_sem.at[0])
    gauge_load = pltpu.make_async_copy(gauge_hbm, gauge, load_sem.at[1])
    source_load.start()
    gauge_load.start()
    barrier = pltpu.get_barrier_semaphore()
    for target in targets:
        pl.semaphore_signal(barrier, inc=1, device_id=target, device_id_type=MESH)

    upper = (2 * gz) // nz
    early, late = 2 + upper, 3 - upper
    early_sign = (1 - 2 * upper).astype(jnp.float32)

    def halo_copy(step, halo, g):
        if isinstance(halo, int):
            target = targets[halo]
        else:
            target = (ta, lax.rem(gz + (3 - halo) * (nz - 1) + (halo - 2), nz))
        return pltpu.make_async_remote_copy(
            src_ref=sent.at[step, halo, g],
            dst_ref=got.at[step, halo, g],
            send_sem=send_sem.at[step, halo, g],
            recv_sem=recv_sem.at[step, halo, g],
            device_id=target,
            device_id_type=MESH,
        )

    def link_copy(which):
        return pltpu.make_async_remote_copy(
            src_ref=gauge_hbm.at[pl.ds(9 * (3 - which), 9)],
            dst_ref=links_below.at[which],
            send_sem=link_send.at[which],
            recv_sem=link_recv.at[which],
            device_id=(above_t, above_z)[which],
            device_id_type=MESH,
        )

    def put_halos(step, g, at):
        for halo, (direction, hop_sign) in enumerate(HALOS):
            half = project(at, direction, hop_sign)
            for s in range(2):
                for c in range(3):
                    sent[step, halo, g, pl.ds((s * 3 + c) * 16, 16)] = half[s][c]

    def rows_of(ri, s, c, g):
        return pl.ds(((ri * 3 + c) * groups + g) * 32 + s, 8, stride=4)

    source_load.wait()
    for p in range(source.shape[0]):
        wide[8 * p : 8 * p + 8] = source[p].astype(jnp.float32)
    for g in range(groups):
        for ri in range(2):
            for s in range(4):
                for c in range(3):
                    psi[0, g, plane(ri, s, c)] = wide[rows_of(ri, s, c, g)]

    def load_psi(step, g):
        return lambda ri, s, c: psi[step, g, plane(ri, s, c)]

    def first_halos(g, carry):
        put_halos(0, g, load_psi(0, g))
        return carry

    lax.fori_loop(0, groups, first_halos, 0)
    pl.semaphore_wait(barrier, 4)
    for which in range(2):
        link_copy(which).start()

    def first_sends(g, carry):
        for halo in (0, 1, late):
            halo_copy(0, halo, g).start()
        return carry

    for g in range(groups):
        halo_copy(0, early, g).start()
    lax.fori_loop(0, groups, first_sends, 0)

    first_half = lax.broadcasted_iota(jnp.int32, (8, LANES), 0) % 2 == 0

    def spread(rows, ri, scale):
        return scale * jnp.where(
            first_half,
            jnp.broadcast_to(rows[ri : ri + 1], (8, LANES)),
            jnp.broadcast_to(rows[2 + ri : 3 + ri], (8, LANES)),
        )

    def put_link(direction, hop_sign, ri, r, c, tile):
        if hop_sign > 0:
            links[link_slot(direction, 1), ri * 9 + r * 3 + c] = tile
        else:
            links[link_slot(direction, -1), ri * 9 + c * 3 + r] = tile if ri == 0 else -tile

    forward_scale = jnp.where(ta == nt - 1, HOPPING, -HOPPING).astype(jnp.float32)
    backward_scale = jnp.where(ta == 0, HOPPING, -HOPPING).astype(jnp.float32)
    gauge_load.wait()
    for direction in range(4):
        scale = forward_scale if direction == 3 else jnp.float32(-HOPPING)
        for r in range(3):
            for c in range(3):
                rows = gauge[direction * 9 + r * 3 + c].astype(jnp.float32)
                for ri in range(2):
                    tile = spread(rows, ri, scale)
                    put_link(direction, 1, ri, r, c, tile)
                    if direction < 2:
                        put_link(direction, -1, ri, r, c, shift_sites(tile, direction, -1))

    def load_link(direction, hop_sign):
        slot = link_slot(direction, hop_sign)
        return lambda ri, r, c: links[slot, ri * 9 + r * 3 + c]

    def load_spinor(at):
        return [[[at(ri, s, c) for c in range(3)] for s in range(4)] for ri in range(2)]

    def plane_hops(step):
        def body(g, carry):
            at = load_psi(step, g)
            total = load_spinor(at)
            for direction in (0, 1):
                for hop_sign in (1, -1):
                    pairs = project(at, direction, hop_sign)
                    half = [
                        [
                            tuple(shift_sites(v, direction, hop_sign) for v in widened(pairs[s][c]))
                            for c in range(3)
                        ]
                        for s in range(2)
                    ]
                    add_hop(total, half, load_link(direction, hop_sign), direction, hop_sign)
            for ri in range(2):
                for s in range(4):
                    for c in range(3):
                        acc[g, plane(ri, s, c)] = total[ri][s][c]
            return carry

        lax.fori_loop(0, groups, body, 0)

    def add_halo(total, step, halo, g, link, direction, hop_sign):
        halo_copy(step, halo, g).wait_recv()
        half = [
            [widened(got[step, halo, g, pl.ds((s * 3 + c) * 16, 16)]) for c in range(3)]
            for s in range(2)
        ]
        add_hop(total, half, link, direction, hop_sign)

    def slot_link(slot):
        return lambda ri, r, c: links[slot, ri * 9 + r * 3 + c]

    def early_hops(g, carry):
        total = load_spinor(lambda ri, s, c: acc[g, plane(ri, s, c)])
        for halo, (direction, hop_sign) in enumerate(HALOS[:2]):
            add_halo(total, 0, halo, g, load_link(direction, hop_sign), direction, hop_sign)
        add_halo(total, 0, early, g, slot_link(4 + upper), 2, early_sign)
        half = project(lambda ri, s, c: total[ri][s][c], 2, early_sign)
        for s in range(2):
            for c in range(3):
                sent[1, early, g, pl.ds((s * 3 + c) * 16, 16)] = half[s][c]
        for ri in range(2):
            for s in range(4):
                for c in range(3):
                    acc[g, plane(ri, s, c)] = total[ri][s][c]
        halo_copy(1, early, g).start()
        return carry

    def halo_hops(step):
        def body(g, carry):
            total = load_spinor(lambda ri, s, c: acc[g, plane(ri, s, c)])
            if step == 0:
                add_halo(total, 0, late, g, slot_link(5 - upper), 2, -early_sign)
            else:
                for halo, (direction, hop_sign) in enumerate(HALOS):
                    add_halo(total, 1, halo, g, load_link(direction, hop_sign), direction, hop_sign)
            final = {}
            for s in range(4):
                for c in range(3):
                    final[0, s, c], final[1, s, c] = widened(
                        rounded(total[0][s][c], total[1][s][c])
                    )
            for (ri, s, c), tile in final.items():
                if step == 0:
                    psi[1, g, plane(ri, s, c)] = tile
                else:
                    wide[rows_of(ri, s, c, g)] = tile
            if step == 0:
                at = lambda ri, s, c: final[ri, s, c]
                halves = (
                    (0, project(at, 3, 1)), (1, project(at, 3, -1)), (late, project(at, 2, -early_sign))
                )
                for halo, half in halves:
                    for s in range(2):
                        for c in range(3):
                            sent[1, halo, g, pl.ds((s * 3 + c) * 16, 16)] = half[s][c]
                for halo, _ in halves:
                    halo_copy(1, halo, g).start()
            else:
                for block in range(6):
                    for p in range(4):
                        at = (block * groups + g) * 4 + p
                        out[at] = wide[pl.ds(8 * at, 8)].astype(jnp.bfloat16)
            return carry

        lax.fori_loop(0, groups, body, 0)

    plane_hops(0)
    for which, scale in ((0, backward_scale), (1, jnp.float32(-HOPPING))):
        link_copy(which).wait_recv()
        for r in range(3):
            for c in range(3):
                rows = links_below[which, r * 3 + c].astype(jnp.float32)
                for ri in range(2):
                    put_link(3 - which, -1, ri, r, c, spread(rows, ri, scale))
    lax.fori_loop(0, groups, early_hops, 0)
    halo_hops(0)
    plane_hops(1)
    halo_hops(1)

    def drain(g, carry):
        for step in range(2):
            for halo in range(4):
                halo_copy(step, halo, g).wait_send()
        return carry

    lax.fori_loop(0, groups, drain, 0)
    for which in range(2):
        link_copy(which).wait_send()


def body(source, gauge_field):
    rhs = source.shape[5]
    groups = rhs // 4
    source_rows = source.reshape(2, 4, 3, rhs, 2, LANES).transpose(0, 2, 3, 4, 1, 5)
    source_rows = source_rows.reshape(6 * rhs, 8, LANES)
    gauge_rows = gauge_field.reshape(4, 2, 3, 3, 2, LANES).transpose(0, 2, 3, 4, 1, 5)
    gauge_rows = gauge_rows.reshape(36, 4, LANES)
    rows = pl.pallas_call(
        functools.partial(kernel, groups),
        out_shape=pltpu.VMEM(source_rows.shape, source.dtype),
        in_specs=[pl.BlockSpec(memory_space=pltpu.HBM)] * 2,
        out_specs=pl.BlockSpec(memory_space=pltpu.VMEM),
        scratch_shapes=[
            pltpu.VMEM(source_rows.shape, jnp.bfloat16),
            pltpu.VMEM(gauge_rows.shape, jnp.bfloat16),
            pltpu.VMEM((48 * rhs, LANES), jnp.float32),
            pltpu.VMEM((2, groups, 24, 8, LANES), jnp.float32),
            pltpu.VMEM((groups, 24, 8, LANES), jnp.float32),
            pltpu.VMEM((8, 18, 8, LANES), jnp.float32),
            pltpu.VMEM((2, 4, groups, 96, LANES), jnp.bfloat16),
            pltpu.VMEM((2, 4, groups, 96, LANES), jnp.bfloat16),
            pltpu.VMEM((2, 9, 4, LANES), jnp.bfloat16),
            pltpu.SemaphoreType.DMA((2,)),
            pltpu.SemaphoreType.DMA((2, 4, groups)),
            pltpu.SemaphoreType.DMA((2, 4, groups)),
            pltpu.SemaphoreType.DMA((2,)),
            pltpu.SemaphoreType.DMA((2,)),
        ],
        compiler_params=pltpu.CompilerParams(collective_id=0, has_side_effects=True),
        name="dirac_twice",
    )(source_rows, gauge_rows)
    out = rows.reshape(2, 3, rhs, 2, 4, LANES).transpose(0, 4, 1, 2, 3, 5)
    return out.reshape(source.shape)


def solution(mesh):
    spec = P("ta", "gz", None, None, None, None, None)
    return jax.shard_map(body, mesh=mesh, in_specs=(spec, spec), out_specs=spec, check_vma=False)
```

profile of v0, /device:TPU:0, one launch (start us, length us, event | category | flops | bytes accessed | tf_op | source)
XLA Modules:
  0.0 14.4 jit_solution(2809965849707864491)
XLA Ops:
  0.0 13.8 %dirac_twice.1 = bf16[72,8,128]{2,1,0:T(8,128)(2,1)S(1)} custom-call(bf16[72,8,128]{2,1,0:T(8,128)(2,1)} %bitcast.16, bf16[36,4,128]{2,1,0:T(4,128)(2,1)} %bitcast.17), custom_call_target="tpu_custom_call" | custom-call | tf_op jit(solution)/shard_map/dirac_twice/pallas_call | solution.py:358
  13.8 0.7 %copy.7 = bf16[1,1,2,4,3,12,256]{6,3,5,4,2,1,0:T(4,128)(2,1)} copy(bf16[1,1,2,4,3,12,256]{6,3,5,4,2,1,0:T(4,128)(2,1)S(1)} %bitcast.15) | data formatting | bytes 294912
where the time goes:
time: 14.6 us; the launch traced here: 14.4 us
  Pallas kernels  13.8 us (95%)
  local copies, waits for them, and re-layouts  0.66 us (5%)
    pallas_call x1, Pallas kernels, body(): pl.pallas_call(functools.partial(kernel, groups), out_shape=pltpu.VMEM(so...  13.8 us
    unnamed x1, local copies, waits for them, and re-layouts  0.66 us

commit v1 on v0

v1 whole, which is shorter than its diff:
```python
import functools

import jax
import jax.numpy as jnp
from jax import lax
from jax.experimental import pallas as pl
from jax.experimental.pallas import tpu as pltpu
from jax.sharding import PartitionSpec as P

NX = 16
HOPPING = 0.124
GAMMA_PERM = ((3, 2, 1, 0), (3, 2, 1, 0), (2, 3, 0, 1), (2, 3, 0, 1))
GAMMA_PHASE = (
    ((0, 1), (0, 1), (0, -1), (0, -1)),
    ((-1, 0), (1, 0), (1, 0), (-1, 0)),
    ((0, 1), (0, -1), (0, -1), (0, 1)),
    ((1, 0), (1, 0), (1, 0), (1, 0)),
)
LANES = 128
MESH = pl.DeviceIdType.MESH
COMPONENTS = [(ri, s, c) for ri in range(2) for s in range(4) for c in range(3)]

HALOS = ((3, 1), (3, -1), (2, 1), (2, -1))


def signed_sum(base, term, sign):
    return base + term if sign > 0 else base - term


def project_row(psi, direction, hop_sign, s):
    partner = GAMMA_PERM[direction][s]
    pr, pi = GAMMA_PHASE[direction][s]
    row = []
    for c in range(3):
        if pi == 0:
            re = signed_sum(psi(0, s, c), psi(0, partner, c), -hop_sign * pr)
            im = signed_sum(psi(1, s, c), psi(1, partner, c), -hop_sign * pr)
        else:
            re = signed_sum(psi(0, s, c), psi(1, partner, c), hop_sign * pi)
            im = signed_sum(psi(1, s, c), psi(0, partner, c), -hop_sign * pi)
        row.append((re, im))
    return row


def color_product(link, row):
    out = []
    for r in range(3):
        re = im = None
        for c in range(3):
            lr, li = link(0, r, c), link(1, r, c)
            hr, hi = row[c]
            tr = lr * hr - li * hi
            ti = lr * hi + li * hr
            re = tr if re is None else re + tr
            im = ti if im is None else im + ti
        out.append((re, im))
    return out


def add_rebuilt(total, row, direction, hop_sign, s):
    low = GAMMA_PERM[direction].index(s)
    pr, pi = GAMMA_PHASE[direction][low]
    for c in range(3):
        kr, ki = row[c]
        total[0, s, c] = total[0, s, c] + kr
        total[1, s, c] = total[1, s, c] + ki
        if pi == 0:
            total[0, low, c] = signed_sum(total[0, low, c], kr, -hop_sign * pr)
            total[1, low, c] = signed_sum(total[1, low, c], ki, -hop_sign * pr)
        else:
            total[0, low, c] = signed_sum(total[0, low, c], ki, hop_sign * pi)
            total[1, low, c] = signed_sum(total[1, low, c], kr, -hop_sign * pi)


def packed(pair):
    return jnp.concatenate(pair, 0).astype(jnp.bfloat16)


def widened(tile):
    wide = tile.astype(jnp.float32)
    return wide[:8], wide[8:]


def shift_sites(tile, direction, steps):
    lane = lax.broadcasted_iota(jnp.int32, (8, LANES), 1)
    if direction == 0:
        column = lane % NX
        if steps > 0:
            return jnp.where(
                column == NX - 1,
                pltpu.roll(tile, NX - 1, axis=1),
                pltpu.roll(tile, LANES - 1, axis=1),
            )
        return jnp.where(
            column == 0,
            pltpu.roll(tile, LANES - (NX - 1), axis=1),
            pltpu.roll(tile, 1, axis=1),
        )
    near = pltpu.roll(tile, LANES - NX if steps > 0 else NX, axis=1)
    first_half = lax.broadcasted_iota(jnp.int32, (8, LANES), 0) % 2 == 0
    other = jnp.where(first_half, pltpu.roll(near, 7, axis=0), pltpu.roll(near, 1, axis=0))
    return jnp.where(lane >= LANES - NX if steps > 0 else lane < NX, other, near)


def plane(ri, s, c):
    return (ri * 4 + s) * 3 + c


def link_slot(direction, hop_sign):
    return direction * 2 + (0 if hop_sign > 0 else 1)


def kernel(
    groups, source_hbm, gauge_hbm, out, source, gauge, wide, psi, acc, links, sent, got,
    load_sem, send_sem, stage_sem, final_sem, ready,
):
    chunks = 2 * groups
    ta, gz = lax.axis_index("ta"), lax.axis_index("gz")
    nt, nz = lax.axis_size("ta"), lax.axis_size("gz")
    above_t = (lax.rem(ta + 1, nt), gz)
    below_t = (lax.rem(ta + nt - 1, nt), gz)
    above_z = (ta, lax.rem(gz + 1, nz))
    below_z = (ta, lax.rem(gz + nz - 1, nz))
    targets = (below_t, above_t, below_z, above_z)

    gauge_load = pltpu.make_async_copy(gauge_hbm, gauge, load_sem.at[0])
    source_load = pltpu.make_async_copy(source_hbm, source, load_sem.at[1])
    gauge_load.start()
    source_load.start()

    barrier = pltpu.get_barrier_semaphore()

    def signal_when(condition, semaphore, target):
        @pl.when(condition)
        def _():
            pl.semaphore_signal(semaphore, inc=1, device_id=target, device_id_type=MESH)

    def wait_for(semaphore, *conditions):
        count = sum(c.astype(jnp.int32) for c in conditions)

        @pl.when(count > 0)
        def _():
            pl.semaphore_wait(semaphore, count)

    first_t, last_t, first_z, last_z = ta == 0, ta == nt - 1, gz == 0, gz == nz - 1
    signal_when(ta < nt - 1, barrier, above_t)
    signal_when(first_t, barrier, below_t)
    signal_when(gz < nz - 1, barrier, above_z)
    signal_when(first_z, barrier, below_z)
    wait_for(barrier, ta > 0, last_t, gz > 0, last_z)
    signal_when(last_z, ready.at[2], above_z)
    signal_when(gz > 0, ready.at[1], below_z)
    signal_when(ta > 0, ready.at[0], below_t)
    signal_when(last_t, ready.at[0], above_t)

    upper = (2 * gz) // nz

    def is_late(halo):
        there = (2 * lax.rem(gz + (nz - 1 if halo == 2 else 1), nz)) // nz
        return there if halo == 2 else 1 - there

    def start_halo(step, halo, q):
        if step == 1:
            slot, semaphore = halo, final_sem.at[q]
        elif halo < 2:
            slot, semaphore = halo, stage_sem.at[0, q]
        else:
            late = is_late(halo)
            slot, semaphore = 2 + late, stage_sem.at[late, q]
        pltpu.make_async_remote_copy(
            src_ref=sent.at[step, halo, q],
            dst_ref=got.at[step, q, slot],
            send_sem=send_sem.at[0],
            recv_sem=semaphore,
            device_id=targets[halo],
            device_id_type=MESH,
        ).start()

    def start_all(*halos):
        def one(q, carry):
            for condition, halo in halos:
                @pl.when(condition)
                def _():
                    start_halo(0, halo, q)
            return carry

        lax.fori_loop(0, chunks, one, 0)

    def landed(ref, semaphore):
        return pltpu.make_async_remote_copy(
            src_ref=ref, dst_ref=ref, send_sem=send_sem.at[0], recv_sem=semaphore,
            device_id=above_t, device_id_type=MESH,
        )

    def load_link(direction, hop_sign):
        slot = link_slot(direction, hop_sign)
        return lambda ri, r, c: links[slot, ri * 9 + r * 3 + c]

    def put_halo(step, halo, q, s, at):
        direction, hop_sign = HALOS[halo]
        row = project_row(at, direction, hop_sign, s)
        if hop_sign < 0:
            row = color_product(load_link(direction, -1), row)
        for c in range(3):
            sent[step, halo, q, 16 * c : 16 * c + 16] = packed(row[c])

    def add_halo(total, step, slot, q, s, halo):
        direction, hop_sign = HALOS[halo]
        row = [widened(got[step, q, slot, 16 * c : 16 * c + 16]) for c in range(3)]
        if hop_sign > 0:
            row = color_product(load_link(direction, 1), row)
        add_rebuilt(total, row, direction, hop_sign, s)

    def rows_of(ri, s, c, g):
        return pl.ds(((ri * 3 + c) * groups + g) * 32 + s, 8, stride=4)

    first_half = lax.broadcasted_iota(jnp.int32, (8, LANES), 0) % 2 == 0

    def spread(rows, ri, scale):
        return scale * jnp.where(
            first_half,
            jnp.broadcast_to(rows[ri : ri + 1], (8, LANES)),
            jnp.broadcast_to(rows[2 + ri : 3 + ri], (8, LANES)),
        )

    def put_links(*directions):
        for direction in directions:
            scale = jnp.float32(-HOPPING)
            if direction == 3:
                scale = jnp.where(last_t, HOPPING, -HOPPING).astype(jnp.float32)
            for r in range(3):
                for c in range(3):
                    rows = gauge[direction * 9 + r * 3 + c].astype(jnp.float32)
                    for ri in range(2):
                        tile = spread(rows, ri, scale)
                        links[link_slot(direction, 1), ri * 9 + r * 3 + c] = tile
                        if direction < 2:
                            tile = shift_sites(tile, direction, -1)
                        links[link_slot(direction, -1), ri * 9 + c * 3 + r] = tile if ri == 0 else -tile

    gauge_load.wait()
    put_links(3, 2)
    source_load.wait()
    for p in range(source.shape[0]):
        wide[8 * p : 8 * p + 8] = source[p].astype(jnp.float32)
    for g in range(groups):
        for ri, s, c in COMPONENTS:
            psi[0, g, plane(ri, s, c)] = wide[rows_of(ri, s, c, g)]

    def load_psi(step, g):
        return lambda ri, s, c: psi[step, g, plane(ri, s, c)]

    def first_halos(g, carry):
        for s in range(2):
            for halo in range(4):
                put_halo(0, halo, 2 * g + s, s, load_psi(0, g))
        return carry

    lax.fori_loop(0, groups, first_halos, 0)
    start_all((last_z, 3), (ta > 0, 0), (last_t, 1))
    start_all((gz > 0, 2))
    wait_for(ready.at[1], gz < nz - 1)
    start_all((gz < nz - 1, 3))
    wait_for(ready.at[0], ta < nt - 1, first_t)
    start_all((ta < nt - 1, 1), (first_t, 0))

    put_links(0, 1)

    def load_acc(g):
        return {at: acc[g, plane(*at)] for at in COMPONENTS}

    def plane_hops(step):
        def body(g, carry):
            at = load_psi(step, g)
            total = {key: at(*key) for key in COMPONENTS}
            for direction in (0, 1):
                for hop_sign in (1, -1):
                    for s in range(2):
                        row = [
                            tuple(shift_sites(v, direction, hop_sign) for v in pair)
                            for pair in project_row(at, direction, hop_sign, s)
                        ]
                        row = color_product(load_link(direction, hop_sign), row)
                        add_rebuilt(total, row, direction, hop_sign, s)
            for key, tile in total.items():
                acc[g, plane(*key)] = tile
            return carry

        lax.fori_loop(0, groups, body, 0)

    plane_hops(0)
    wait_for(ready.at[2], first_z)
    start_all((first_z, 2))

    def stages(near, far):
        def early(g, carry):
            for s in range(2):
                q = 2 * g + s
                total = {k: acc[g, plane(*k)] for k in COMPONENTS if k[1] in (s, s + 2)}
                landed(got.at[0, q, pl.ds(0, 3)], stage_sem.at[0, q]).wait_recv()
                add_halo(total, 0, 0, q, s, 0)
                add_halo(total, 0, 1, q, s, 1)
                add_halo(total, 0, 2, q, s, near)
                put_halo(1, near, q, s, lambda *k: total[k])
                start_halo(1, near, q)
                for k, tile in total.items():
                    acc[g, plane(*k)] = tile
            return carry

        def late(g, carry):
            for s in range(2):
                q = 2 * g + s
                total = {k: acc[g, plane(*k)] for k in COMPONENTS if k[1] in (s, s + 2)}
                landed(got.at[0, q, 3], stage_sem.at[1, q]).wait_recv()
                add_halo(total, 0, 3, q, s, far)
                for s2 in (s, s + 2):
                    for c in range(3):
                        total[0, s2, c], total[1, s2, c] = widened(
                            packed([total[0, s2, c], total[1, s2, c]])
                        )
                for halo in (0, 1, far):
                    put_halo(1, halo, q, s, lambda *k: total[k])
                for halo in (0, 1, far):
                    start_halo(1, halo, q)
                for k, tile in total.items():
                    psi[1, g, plane(*k)] = tile
            return carry

        lax.fori_loop(0, groups, early, 0)
        lax.fori_loop(0, groups, late, 0)

    @pl.when(upper == 0)
    def _():
        stages(2, 3)

    @pl.when(upper == 1)
    def _():
        stages(3, 2)

    plane_hops(1)

    def last(g, carry):
        for s in range(2):
            q = 2 * g + s
            total = {k: acc[g, plane(*k)] for k in COMPONENTS if k[1] in (s, s + 2)}
            landed(got.at[1, q], final_sem.at[q]).wait_recv()
            for halo in range(4):
                add_halo(total, 1, halo, q, s, halo)
            for (ri, s2, c), tile in total.items():
                wide[rows_of(ri, s2, c, g)] = tile
        for block in range(6):
            for p in range(4):
                at = (block * groups + g) * 4 + p
                out[at] = wide[pl.ds(8 * at, 8)].astype(jnp.bfloat16)
        return carry

    lax.fori_loop(0, groups, last, 0)
    landed(sent, stage_sem.at[0, 0]).wait_send()


def body(source, gauge_field):
    rhs = source.shape[5]
    groups = rhs // 4
    chunks = 2 * groups
    source_rows = source.reshape(2, 4, 3, rhs, 2, LANES).transpose(0, 2, 3, 4, 1, 5)
    source_rows = source_rows.reshape(6 * rhs, 8, LANES)
    gauge_rows = gauge_field.reshape(4, 2, 3, 3, 2, LANES).transpose(0, 2, 3, 4, 1, 5)
    gauge_rows = gauge_rows.reshape(36, 4, LANES)
    rows = pl.pallas_call(
        functools.partial(kernel, groups),
        out_shape=pltpu.VMEM(source_rows.shape, source.dtype),
        in_specs=[pl.BlockSpec(memory_space=pltpu.HBM)] * 2,
        out_specs=pl.BlockSpec(memory_space=pltpu.VMEM),
        scratch_shapes=[
            pltpu.VMEM(source_rows.shape, jnp.bfloat16),
            pltpu.VMEM(gauge_rows.shape, jnp.bfloat16),
            pltpu.VMEM((48 * rhs, LANES), jnp.float32),
            pltpu.VMEM((2, groups, 24, 8, LANES), jnp.float32),
            pltpu.VMEM((groups, 24, 8, LANES), jnp.float32),
            pltpu.VMEM((8, 18, 8, LANES), jnp.float32),
            pltpu.VMEM((2, 4, chunks, 48, LANES), jnp.bfloat16),
            pltpu.VMEM((2, chunks, 4, 48, LANES), jnp.bfloat16),
            pltpu.SemaphoreType.DMA((2,)),
            pltpu.SemaphoreType.DMA((1,)),
            pltpu.SemaphoreType.DMA((2, chunks)),
            pltpu.SemaphoreType.DMA((chunks,)),
            pltpu.SemaphoreType.REGULAR((3,)),
        ],
        compiler_params=pltpu.CompilerParams(collective_id=0, has_side_effects=True),
        name="dirac_twice",
    )(source_rows, gauge_rows)
    out = rows.reshape(2, 3, rhs, 2, 4, LANES).transpose(0, 4, 1, 2, 3, 5)
    return out.reshape(source.shape)


def solution(mesh):
    spec = P("ta", "gz", None, None, None, None, None)
    return jax.shard_map(body, mesh=mesh, in_specs=(spec, spec), out_specs=spec, check_vma=False)
```

time: 14.6 us -> 14 us (0.959)
  the two profiles are of different devices: /device:TPU:0 before, /device:TPU:4 now
where the time goes in v1:
time: 14 us; the launch traced here: 13.8 us
  Pallas kernels  13.2 us (94%)
  local copies, waits for them, and re-layouts  0.66 us (5%)
    pallas_call x1, Pallas kernels, body(): pl.pallas_call(functools.partial(kernel, groups), out_shape=pltpu.VMEM(so...  13.2 us
    unnamed x1, local copies, waits for them, and re-layouts  0.66 us

profile of v1, /device:TPU:4, one launch (start us, length us, event | category | flops | bytes accessed | tf_op | source)
XLA Modules:
  0.0 13.8 jit_solution(1932878071311702329)
XLA Ops:
  0.0 13.2 %dirac_twice.1 = bf16[72,8,128]{2,1,0:T(8,128)(2,1)S(1)} custom-call(bf16[72,8,128]{2,1,0:T(8,128)(2,1)} %bitcast.16, bf16[36,4,128]{2,1,0:T(4,128)(2,1)} %bitcast.17), custom_call_target="tpu_custom_call" | custom-call | tf_op jit(solution)/shard_map/dirac_twice/pallas_call | solution.py:369
  13.2 0.7 %copy.7 = bf16[1,1,2,4,3,12,256]{6,3,5,4,2,1,0:T(4,128)(2,1)} copy(bf16[1,1,2,4,3,12,256]{6,3,5,4,2,1,0:T(4,128)(2,1)S(1)} %bitcast.15) | data formatting | bytes 294912

commit v2 on v1

--- a/solution.py
+++ b/solution.py
@@ -123,10 +123,33 @@
     below_z = (ta, lax.rem(gz + nz - 1, nz))
     targets = (below_t, above_t, below_z, above_z)
 
-    gauge_load = pltpu.make_async_copy(gauge_hbm, gauge, load_sem.at[0])
-    source_load = pltpu.make_async_copy(source_hbm, source, load_sem.at[1])
-    gauge_load.start()
-    source_load.start()
+    def block_loads(g):
+        rows = groups * 4
+        return [
+            pltpu.make_async_copy(
+                source_hbm.at[pl.ds(block * rows + 4 * g, 4)],
+                source.at[pl.ds(block * rows + 4 * g, 4)],
+                load_sem.at[g],
+            )
+            for block in range(6)
+        ]
+
+    def source_group(g):
+        return pltpu.make_async_copy(
+            source_hbm.at[pl.ds(0, 24)], source.at[pl.ds(0, 24)], load_sem.at[g]
+        )
+
+    far_gauge = pltpu.make_async_copy(
+        gauge_hbm.at[pl.ds(18, 18)], gauge.at[pl.ds(18, 18)], load_sem.at[groups]
+    )
+    near_gauge = pltpu.make_async_copy(
+        gauge_hbm.at[pl.ds(0, 18)], gauge.at[pl.ds(0, 18)], load_sem.at[groups + 1]
+    )
+    far_gauge.start()
+    for g in range(groups):
+        for load in block_loads(g):
+            load.start()
+    near_gauge.start()
 
     barrier = pltpu.get_barrier_semaphore()
 
@@ -143,15 +166,19 @@
             pl.semaphore_wait(semaphore, count)
 
     first_t, last_t, first_z, last_z = ta == 0, ta == nt - 1, gz == 0, gz == nz - 1
-    signal_when(ta < nt - 1, barrier, above_t)
-    signal_when(first_t, barrier, below_t)
-    signal_when(gz < nz - 1, barrier, above_z)
-    signal_when(first_z, barrier, below_z)
-    wait_for(barrier, ta > 0, last_t, gz > 0, last_z)
-    signal_when(last_z, ready.at[2], above_z)
-    signal_when(gz > 0, ready.at[1], below_z)
-    signal_when(ta > 0, ready.at[0], below_t)
-    signal_when(last_t, ready.at[0], above_t)
+    stands_back = (lax.rem(ta, 2) == 1) & (ta > 1) & ~last_t
+    even, odd = lax.rem(ta, 2) == 0, lax.rem(ta, 2) == 1
+    met_below_t, met_above_t = (ta > 0) & (ta != nt // 2), last_t | (ta == nt // 2 - 1)
+    met_below_z, met_above_z = ~first_z, last_z
+    signal_when(~met_above_t, barrier, above_t)
+    signal_when(~met_below_t, barrier, below_t)
+    signal_when(~met_above_z, barrier, above_z)
+    signal_when(~met_below_z, barrier, below_z)
+    wait_for(barrier, met_below_t, met_above_t, met_below_z, met_above_z)
+    signal_when(met_above_z, ready.at[2], above_z)
+    signal_when(met_below_z, ready.at[1], below_z)
+    signal_when(met_below_t, ready.at[0], below_t)
+    signal_when(met_above_t, ready.at[0], above_t)
 
     upper = (2 * gz) // nz
 
@@ -176,12 +203,12 @@
             device_id_type=MESH,
         ).start()
 
-    def start_all(*halos):
+    def start_all(*halos, step=0):
         def one(q, carry):
             for condition, halo in halos:
                 @pl.when(condition)
                 def _():
-                    start_halo(0, halo, q)
+                    start_halo(step, halo, q)
             return carry
 
         lax.fori_loop(0, chunks, one, 0)
@@ -238,32 +265,40 @@
                             tile = shift_sites(tile, direction, -1)
                         links[link_slot(direction, -1), ri * 9 + c * 3 + r] = tile if ri == 0 else -tile
 
-    gauge_load.wait()
-    put_links(3, 2)
-    source_load.wait()
-    for p in range(source.shape[0]):
-        wide[8 * p : 8 * p + 8] = source[p].astype(jnp.float32)
-    for g in range(groups):
-        for ri, s, c in COMPONENTS:
-            psi[0, g, plane(ri, s, c)] = wide[rows_of(ri, s, c, g)]
-
     def load_psi(step, g):
         return lambda ri, s, c: psi[step, g, plane(ri, s, c)]
 
-    def first_halos(g, carry):
-        for s in range(2):
-            for halo in range(4):
-                put_halo(0, halo, 2 * g + s, s, load_psi(0, g))
-        return carry
-
-    lax.fori_loop(0, groups, first_halos, 0)
-    start_all((last_z, 3), (ta > 0, 0), (last_t, 1))
-    start_all((gz > 0, 2))
-    wait_for(ready.at[1], gz < nz - 1)
-    start_all((gz < nz - 1, 3))
-    wait_for(ready.at[0], ta < nt - 1, first_t)
-    start_all((ta < nt - 1, 1), (first_t, 0))
-
+    def start_when(condition, halo, g):
+        @pl.when(condition)
+        def _():
+            for s in range(2):
+                start_halo(0, halo, 2 * g + s)
+
+    far_gauge.wait()
+    put_links(3, 2)
+    for g in range(groups):
+        source_group(g).wait()
+        for block in range(6):
+            for p in range(4):
+                at = (block * groups + g) * 4 + p
+                wide[8 * at : 8 * at + 8] = source[at].astype(jnp.float32)
+        tiles = {(ri, s, c): wide[rows_of(ri, s, c, g)] for ri, s, c in COMPONENTS}
+        for halo in range(4):
+            for s in range(2):
+                put_halo(0, halo, 2 * g + s, s, lambda *k: tiles[k])
+        for k, tile in tiles.items():
+            psi[0, g, plane(*k)] = tile
+        start_when(last_z & ~stands_back, 3, g)
+        start_when(met_below_t, 0, g)
+        start_when(met_above_t, 1, g)
+    start_all((met_below_z, 2))
+    wait_for(ready.at[1], ~met_above_z)
+    start_all((~met_above_z, 3))
+    wait_for(ready.at[0], ~met_above_t, ~met_below_t)
+    start_all((~met_above_t, 1), (~met_below_t, 0))
+    start_all((last_z & stands_back, 3))
+
+    near_gauge.wait()
     put_links(0, 1)
 
     def load_acc(g):
@@ -380,7 +415,7 @@
             pltpu.VMEM((8, 18, 8, LANES), jnp.float32),
             pltpu.VMEM((2, 4, chunks, 48, LANES), jnp.bfloat16),
             pltpu.VMEM((2, chunks, 4, 48, LANES), jnp.bfloat16),
-            pltpu.SemaphoreType.DMA((2,)),
+            pltpu.SemaphoreType.DMA((groups + 2,)),
             pltpu.SemaphoreType.DMA((1,)),
             pltpu.SemaphoreType.DMA((2, chunks)),
             pltpu.SemaphoreType.DMA((chunks,)),

time: 14 us -> 13.5 us (0.964)
  the two profiles are of different devices: /device:TPU:4 before, /device:TPU:0 now
where the time goes in v2:
time: 13.5 us; the launch traced here: 13.3 us
  Pallas kernels  12.7 us (94%)
  local copies, waits for them, and re-layouts  0.66 us (5%)
    pallas_call x1, Pallas kernels, body(): pl.pallas_call(functools.partial(kernel, groups), out_shape=pltpu.VMEM(so...  12.7 us
    unnamed x1, local copies, waits for them, and re-layouts  0.66 us

profile of v2, /device:TPU:0, one launch (start us, length us, event | category | flops | bytes accessed | tf_op | source)
XLA Modules:
  0.0 13.3 jit_solution(3850810413561483214)
XLA Ops:
  0.0 12.7 %dirac_twice.1 = bf16[72,8,128]{2,1,0:T(8,128)(2,1)S(1)} custom-call(bf16[72,8,128]{2,1,0:T(8,128)(2,1)} %bitcast.16, bf16[36,4,128]{2,1,0:T(4,128)(2,1)} %bitcast.17), custom_call_target="tpu_custom_call" | custom-call | tf_op jit(solution)/shard_map/dirac_twice/pallas_call | solution.py:404
  12.7 0.7 %copy.7 = bf16[1,1,2,4,3,12,256]{6,3,5,4,2,1,0:T(4,128)(2,1)} copy(bf16[1,1,2,4,3,12,256]{6,3,5,4,2,1,0:T(4,128)(2,1)S(1)} %bitcast.15) | data formatting | bytes 294912

commit v3 on v1

v3 whole, which is shorter than its diff:
```python
import functools

import jax
import jax.numpy as jnp
from jax import lax
from jax.experimental import pallas as pl
from jax.experimental.pallas import tpu as pltpu
from jax.sharding import PartitionSpec as P

NX = 16
HOPPING = 0.124
GAMMA_PERM = ((3, 2, 1, 0), (3, 2, 1, 0), (2, 3, 0, 1), (2, 3, 0, 1))
GAMMA_PHASE = (
    ((0, 1), (0, 1), (0, -1), (0, -1)),
    ((-1, 0), (1, 0), (1, 0), (-1, 0)),
    ((0, 1), (0, -1), (0, -1), (0, 1)),
    ((1, 0), (1, 0), (1, 0), (1, 0)),
)
LANES = 128
MESH = pl.DeviceIdType.MESH
COMPONENTS = [(ri, s, c) for ri in range(2) for s in range(4) for c in range(3)]

HALOS = ((3, 1), (3, -1), (2, 1), (2, -1))


def signed_sum(base, term, sign):
    return base + term if sign > 0 else base - term


def project_row(psi, direction, hop_sign, s):
    partner = GAMMA_PERM[direction][s]
    pr, pi = GAMMA_PHASE[direction][s]
    row = []
    for c in range(3):
        if pi == 0:
            re = signed_sum(psi(0, s, c), psi(0, partner, c), -hop_sign * pr)
            im = signed_sum(psi(1, s, c), psi(1, partner, c), -hop_sign * pr)
        else:
            re = signed_sum(psi(0, s, c), psi(1, partner, c), hop_sign * pi)
            im = signed_sum(psi(1, s, c), psi(0, partner, c), -hop_sign * pi)
        row.append((re, im))
    return row


def color_product(link, row):
    out = []
    for r in range(3):
        re = im = None
        for c in range(3):
            lr, li = link(0, r, c), link(1, r, c)
            hr, hi = row[c]
            tr = lr * hr - li * hi
            ti = lr * hi + li * hr
            re = tr if re is None else re + tr
            im = ti if im is None else im + ti
        out.append((re, im))
    return out


def add_rebuilt(total, row, direction, hop_sign, s):
    low = GAMMA_PERM[direction].index(s)
    pr, pi = GAMMA_PHASE[direction][low]
    for c in range(3):
        kr, ki = row[c]
        total[0, s, c] = total[0, s, c] + kr
        total[1, s, c] = total[1, s, c] + ki
        if pi == 0:
            total[0, low, c] = signed_sum(total[0, low, c], kr, -hop_sign * pr)
            total[1, low, c] = signed_sum(total[1, low, c], ki, -hop_sign * pr)
        else:
            total[0, low, c] = signed_sum(total[0, low, c], ki, hop_sign * pi)
            total[1, low, c] = signed_sum(total[1, low, c], kr, -hop_sign * pi)


def packed(pair):
    return jnp.concatenate(pair, 0).astype(jnp.bfloat16)


def widened(tile):
    wide = tile.astype(jnp.float32)
    return wide[:8], wide[8:]


def shift_sites(tile, direction, steps):
    lane = lax.broadcasted_iota(jnp.int32, (8, LANES), 1)
    if direction == 0:
        column = lane % NX
        if steps > 0:
            return jnp.where(
                column == NX - 1,
                pltpu.roll(tile, NX - 1, axis=1),
                pltpu.roll(tile, LANES - 1, axis=1),
            )
        return jnp.where(
            column == 0,
            pltpu.roll(tile, LANES - (NX - 1), axis=1),
            pltpu.roll(tile, 1, axis=1),
        )
    near = pltpu.roll(tile, LANES - NX if steps > 0 else NX, axis=1)
    first_half = lax.broadcasted_iota(jnp.int32, (8, LANES), 0) % 2 == 0
    other = jnp.where(first_half, pltpu.roll(near, 7, axis=0), pltpu.roll(near, 1, axis=0))
    return jnp.where(lane >= LANES - NX if steps > 0 else lane < NX, other, near)


def plane(ri, s, c):
    return (ri * 4 + s) * 3 + c


def link_slot(direction, hop_sign):
    return direction * 2 + (0 if hop_sign > 0 else 1)


def kernel(
    groups, source_hbm, gauge_hbm, out, source, gauge, wide, psi, acc, links, sent, got,
    send_sem, final_sem,
):
    chunks = 2 * groups
    ta, gz = lax.axis_index("ta"), lax.axis_index("gz")
    nt, nz = lax.axis_size("ta"), lax.axis_size("gz")
    above_t = (lax.rem(ta + 1, nt), gz)
    below_t = (lax.rem(ta + nt - 1, nt), gz)
    above_z = (ta, lax.rem(gz + 1, nz))
    below_z = (ta, lax.rem(gz + nz - 1, nz))
    targets = (below_t, above_t, below_z, above_z)

    def landed(ref, semaphore):
        return pltpu.make_async_remote_copy(
            src_ref=ref, dst_ref=ref, send_sem=send_sem.at[0], recv_sem=semaphore,
            device_id=above_t, device_id_type=MESH,
        )

    def load_link(direction, hop_sign):
        slot = link_slot(direction, hop_sign)
        return lambda ri, r, c: links[slot, ri * 9 + r * 3 + c]

    def add_halo(total, step, slot, q, s, halo):
        direction, hop_sign = HALOS[halo]
        row = [widened(got[step, q, slot, 16 * c : 16 * c + 16]) for c in range(3)]
        if hop_sign > 0:
            row = color_product(load_link(direction, 1), row)
        add_rebuilt(total, row, direction, hop_sign, s)

    def rows_of(ri, s, c, g):
        return pl.ds(((ri * 3 + c) * groups + g) * 32 + s, 8, stride=4)

    def load_psi(step, g):
        return lambda ri, s, c: psi[step, g, plane(ri, s, c)]

    def plane_hops(step):
        def body(g, carry):
            at = load_psi(step, g)
            total = {key: at(*key) for key in COMPONENTS}
            for direction in (0, 1):
                for hop_sign in (1, -1):
                    for s in range(2):
                        row = [
                            tuple(shift_sites(v, direction, hop_sign) for v in pair)
                            for pair in project_row(at, direction, hop_sign, s)
                        ]
                        row = color_product(load_link(direction, hop_sign), row)
                        add_rebuilt(total, row, direction, hop_sign, s)
            for key, tile in total.items():
                acc[g, plane(*key)] = tile
            return carry

        lax.fori_loop(0, groups, body, 0)

    def first_application(load_sem, stage_sem, ready):
        def block_loads(g):
            rows = groups * 4
            return [
                pltpu.make_async_copy(
                    source_hbm.at[pl.ds(block * rows + 4 * g, 4)],
                    source.at[pl.ds(block * rows + 4 * g, 4)],
                    load_sem.at[g],
                )
                for block in range(6)
            ]

        def source_group(g):
            return pltpu.make_async_copy(
                source_hbm.at[pl.ds(0, 24)], source.at[pl.ds(0, 24)], load_sem.at[g]
            )

        far_gauge = pltpu.make_async_copy(
            gauge_hbm.at[pl.ds(18, 18)], gauge.at[pl.ds(18, 18)], load_sem.at[groups]
        )
        near_gauge = pltpu.make_async_copy(
            gauge_hbm.at[pl.ds(0, 18)], gauge.at[pl.ds(0, 18)], load_sem.at[groups + 1]
        )
        far_gauge.start()
        for g in range(groups):
            for load in block_loads(g):
                load.start()
        near_gauge.start()

        barrier = pltpu.get_barrier_semaphore()

        def signal_when(condition, semaphore, target):
            @pl.when(condition)
            def _():
                pl.semaphore_signal(semaphore, inc=1, device_id=target, device_id_type=MESH)

        def wait_for(semaphore, *conditions):
            count = sum(c.astype(jnp.int32) for c in conditions)

            @pl.when(count > 0)
            def _():
                pl.semaphore_wait(semaphore, count)

        first_t, last_t, first_z, last_z = ta == 0, ta == nt - 1, gz == 0, gz == nz - 1
        stands_back = (lax.rem(ta, 2) == 1) & (ta > 1) & ~last_t
        even, odd = lax.rem(ta, 2) == 0, lax.rem(ta, 2) == 1
        met_below_t, met_above_t = (ta > 0) & (ta != nt // 2), last_t | (ta == nt // 2 - 1)
        met_below_z, met_above_z = ~first_z, last_z
        signal_when(~met_above_t, barrier, above_t)
        signal_when(~met_below_t, barrier, below_t)
        signal_when(~met_above_z, barrier, above_z)
        signal_when(~met_below_z, barrier, below_z)
        wait_for(barrier, met_below_t, met_above_t, met_below_z, met_above_z)
        signal_when(met_above_z, ready.at[2], above_z)
        signal_when(met_below_z, ready.at[1], below_z)
        signal_when(met_below_t, ready.at[0], below_t)
        signal_when(met_above_t, ready.at[0], above_t)

        upper = (2 * gz) // nz

        def is_late(halo):
            there = (2 * lax.rem(gz + (nz - 1 if halo == 2 else 1), nz)) // nz
            return there if halo == 2 else 1 - there

        def start_halo(step, halo, q):
            if step == 1:
                slot, semaphore = halo, final_sem.at[jnp.maximum(q - (chunks - 3), 0)]
            elif halo < 2:
                slot, semaphore = halo, stage_sem.at[0, q]
            else:
                late = is_late(halo)
                slot, semaphore = 2 + late, stage_sem.at[late, q]
            pltpu.make_async_remote_copy(
                src_ref=sent.at[step, halo, q],
                dst_ref=got.at[step, q, slot],
                send_sem=send_sem.at[0],
                recv_sem=semaphore,
                device_id=targets[halo],
                device_id_type=MESH,
            ).start()

        def start_all(*halos, step=0):
            def one(q, carry):
                for condition, halo in halos:
                    @pl.when(condition)
                    def _():
                        start_halo(step, halo, q)
                return carry

            lax.fori_loop(0, chunks, one, 0)

        def put_halo(step, halo, q, s, at):
            direction, hop_sign = HALOS[halo]
            row = project_row(at, direction, hop_sign, s)
            if hop_sign < 0:
                row = color_product(load_link(direction, -1), row)
            for c in range(3):
                sent[step, halo, q, 16 * c : 16 * c + 16] = packed(row[c])

        first_half = lax.broadcasted_iota(jnp.int32, (8, LANES), 0) % 2 == 0

        def spread(rows, ri, scale):
            return scale * jnp.where(
                first_half,
                jnp.broadcast_to(rows[ri : ri + 1], (8, LANES)),
                jnp.broadcast_to(rows[2 + ri : 3 + ri], (8, LANES)),
            )

        def put_links(*directions):
            for direction in directions:
                scale = jnp.float32(-HOPPING)
                if direction == 3:
                    scale = jnp.where(last_t, HOPPING, -HOPPING).astype(jnp.float32)
                for r in range(3):
                    for c in range(3):
                        rows = gauge[direction * 9 + r * 3 + c].astype(jnp.float32)
                        for ri in range(2):
                            tile = spread(rows, ri, scale)
                            links[link_slot(direction, 1), ri * 9 + r * 3 + c] = tile
                            if direction < 2:
                                tile = shift_sites(tile, direction, -1)
                            links[link_slot(direction, -1), ri * 9 + c * 3 + r] = tile if ri == 0 else -tile

        def start_when(condition, halo, g):
            @pl.when(condition)
            def _():
                for s in range(2):
                    start_halo(0, halo, 2 * g + s)

        far_gauge.wait()
        put_links(3, 2)
        for g in range(groups):
            source_group(g).wait()
            for block in range(6):
                for p in range(4):
                    at = (block * groups + g) * 4 + p
                    wide[8 * at : 8 * at + 8] = source[at].astype(jnp.float32)
            tiles = {(ri, s, c): wide[rows_of(ri, s, c, g)] for ri, s, c in COMPONENTS}
            for halo in range(4):
                for s in range(2):
                    put_halo(0, halo, 2 * g + s, s, lambda *k: tiles[k])
            for k, tile in tiles.items():
                psi[0, g, plane(*k)] = tile
            start_when(last_z & ~stands_back, 3, g)
            start_when(met_below_z & ~last_z, 2, g)
            start_when(met_below_t, 0, g)
            start_when(met_above_t, 1, g)
        start_all((last_z, 2))
        wait_for(ready.at[1], ~met_above_z)
        start_all((~met_above_z, 3))
        wait_for(ready.at[0], ~met_above_t, ~met_below_t)
        start_all((~met_above_t, 1), (~met_below_t, 0))
        start_all((last_z & stands_back, 3))

        near_gauge.wait()
        put_links(0, 1)

        plane_hops(0)
        wait_for(ready.at[2], first_z)
        start_all((first_z, 2))

        def stages(near, far):
            def early(g, carry):
                for s in range(2):
                    q = 2 * g + s
                    total = {k: acc[g, plane(*k)] for k in COMPONENTS if k[1] in (s, s + 2)}
                    landed(got.at[0, q, pl.ds(0, 3)], stage_sem.at[0, q]).wait_recv()
                    add_halo(total, 0, 0, q, s, 0)
                    add_halo(total, 0, 1, q, s, 1)
                    add_halo(total, 0, 2, q, s, near)
                    put_halo(1, near, q, s, lambda *k: total[k])
                    start_halo(1, near, q)
                    for k, tile in total.items():
                        acc[g, plane(*k)] = tile
                return carry

            def late(g, carry):
                for s in range(2):
                    q = 2 * g + s
                    total = {k: acc[g, plane(*k)] for k in COMPONENTS if k[1] in (s, s + 2)}
                    landed(got.at[0, q, 3], stage_sem.at[1, q]).wait_recv()
                    add_halo(total, 0, 3, q, s, far)
                    for s2 in (s, s + 2):
                        for c in range(3):
                            total[0, s2, c], total[1, s2, c] = widened(
                                packed([total[0, s2, c], total[1, s2, c]])
                            )
                    for halo in (0, 1, far):
                        put_halo(1, halo, q, s, lambda *k: total[k])
                    for halo in (0, 1, far):
                        start_halo(1, halo, q)
                    for k, tile in total.items():
                        psi[1, g, plane(*k)] = tile
                return carry

            lax.fori_loop(0, groups, early, 0)
            lax.fori_loop(0, groups, late, 0)

        @pl.when(upper == 0)
        def _():
            stages(2, 3)

        @pl.when(upper == 1)
        def _():
            stages(3, 2)

    pl.run_scoped(
        first_application,
        pltpu.SemaphoreType.DMA((groups + 2,)),
        pltpu.SemaphoreType.DMA((2, chunks)),
        pltpu.SemaphoreType.REGULAR((3,)),
    )
    plane_hops(1)

    for g in range(groups):
        for s in range(2):
            q = 2 * g + s
            total = {k: acc[g, plane(*k)] for k in COMPONENTS if k[1] in (s, s + 2)}
            if q == 0:
                landed(got.at[1, pl.ds(0, chunks - 2)], final_sem.at[0]).wait_recv()
            elif q > chunks - 3:
                landed(got.at[1, q], final_sem.at[q - (chunks - 3)]).wait_recv()
            for halo in range(4):
                add_halo(total, 1, halo, q, s, halo)
            for (ri, s2, c), tile in total.items():
                wide[rows_of(ri, s2, c, g)] = tile
        for block in range(6):
            for p in range(4):
                at = (block * groups + g) * 4 + p
                out[at] = wide[pl.ds(8 * at, 8)].astype(jnp.bfloat16)
    landed(sent, final_sem.at[0]).wait_send()


def body(source, gauge_field):
    rhs = source.shape[5]
    groups = rhs // 4
    chunks = 2 * groups
    source_rows = source.reshape(2, 4, 3, rhs, 2, LANES).transpose(0, 2, 3, 4, 1, 5)
    source_rows = source_rows.reshape(6 * rhs, 8, LANES)
    gauge_rows = gauge_field.reshape(4, 2, 3, 3, 2, LANES).transpose(0, 2, 3, 4, 1, 5)
    gauge_rows = gauge_rows.reshape(36, 4, LANES)
    rows = pl.pallas_call(
        functools.partial(kernel, groups),
        out_shape=pltpu.VMEM(source_rows.shape, source.dtype),
        in_specs=[pl.BlockSpec(memory_space=pltpu.HBM)] * 2,
        out_specs=pl.BlockSpec(memory_space=pltpu.VMEM),
        scratch_shapes=[
            pltpu.VMEM(source_rows.shape, jnp.bfloat16),
            pltpu.VMEM(gauge_rows.shape, jnp.bfloat16),
            pltpu.VMEM((48 * rhs, LANES), jnp.float32),
            pltpu.VMEM((2, groups, 24, 8, LANES), jnp.float32),
            pltpu.VMEM((groups, 24, 8, LANES), jnp.float32),
            pltpu.VMEM((8, 18, 8, LANES), jnp.float32),
            pltpu.VMEM((2, 4, chunks, 48, LANES), jnp.bfloat16),
            pltpu.VMEM((2, chunks, 4, 48, LANES), jnp.bfloat16),
            pltpu.SemaphoreType.DMA((1,)),
            pltpu.SemaphoreType.DMA((3,)),
        ],
        compiler_params=pltpu.CompilerParams(collective_id=0, has_side_effects=True),
        name="dirac_twice",
    )(source_rows, gauge_rows)
    out = rows.reshape(2, 3, rhs, 2, 4, LANES).transpose(0, 4, 1, 2, 3, 5)
    return out.reshape(source.shape)


def solution(mesh):
    spec = P("ta", "gz", None, None, None, None, None)
    return jax.shard_map(body, mesh=mesh, in_specs=(spec, spec), out_specs=spec, check_vma=False)
```

time: 14 us -> 13.3 us (0.950)
  the two profiles are of different devices: /device:TPU:4 before, /device:TPU:0 now
where the time goes in v3:
time: 13.3 us; the launch traced here: 13.2 us
  Pallas kernels  12.5 us (94%)
  local copies, waits for them, and re-layouts  0.66 us (5%)
    pallas_call x1, Pallas kernels, body(): pl.pallas_call(functools.partial(kernel, groups), out_shape=pltpu.VMEM(so...  12.5 us
    unnamed x1, local copies, waits for them, and re-layouts  0.66 us

profile of v3, /device:TPU:0, one launch (start us, length us, event | category | flops | bytes accessed | tf_op | source)
XLA Modules:
  0.0 13.2 jit_solution(2876881935185385644)
XLA Ops:
  0.0 12.5 %dirac_twice.1 = bf16[72,8,128]{2,1,0:T(8,128)(2,1)S(1)} custom-call(bf16[72,8,128]{2,1,0:T(8,128)(2,1)} %bitcast.16, bf16[36,4,128]{2,1,0:T(4,128)(2,1)} %bitcast.17), custom_call_target="tpu_custom_call" | custom-call | tf_op jit(solution)/shard_map/dirac_twice/pallas_call | solution.py:409
  12.5 0.7 %copy.7 = bf16[1,1,2,4,3,12,256]{6,3,5,4,2,1,0:T(4,128)(2,1)} copy(bf16[1,1,2,4,3,12,256]{6,3,5,4,2,1,0:T(4,128)(2,1)S(1)} %bitcast.15) | data formatting | bytes 294912

commit v4 on v3

--- a/solution.py
+++ b/solution.py
@@ -326,6 +326,8 @@
         wait_for(ready.at[2], first_z)
         start_all((first_z, 2))
 
+        held = last_z & (ta == 1)
+
         def stages(near, far):
             def early(g, carry):
                 for s in range(2):
@@ -336,7 +338,12 @@
                     add_halo(total, 0, 1, q, s, 1)
                     add_halo(total, 0, 2, q, s, near)
                     put_halo(1, near, q, s, lambda *k: total[k])
-                    start_halo(1, near, q)
+                    if near == 3:
+                        @pl.when(~held)
+                        def _():
+                            start_halo(1, near, q)
+                    else:
+                        start_halo(1, near, q)
                     for k, tile in total.items():
                         acc[g, plane(*k)] = tile
                 return carry
@@ -361,6 +368,8 @@
                 return carry
 
             lax.fori_loop(0, groups, early, 0)
+            if near == 3:
+                start_all((held, 3), step=1)
             lax.fori_loop(0, groups, late, 0)
 
         @pl.when(upper == 0)

time: 13.3 us -> 12.9 us (0.970)
  Pallas kernels: 12.5 us -> 12.1 us
    pallas_call x1, Pallas kernels: 12.5 us -> 12.1 us  [body(): pl.pallas_call(functools.partial(kernel, groups), out_shape=pltpu.VMEM(so...]
where the time goes in v4:
time: 12.9 us; the launch traced here: 12.7 us
  Pallas kernels  12.1 us (94%)
  local copies, waits for them, and re-layouts  0.66 us (5%)
    pallas_call x1, Pallas kernels, body(): pl.pallas_call(functools.partial(kernel, groups), out_shape=pltpu.VMEM(so...  12.1 us
    unnamed x1, local copies, waits for them, and re-layouts  0.66 us

profile of v4, /device:TPU:0, one launch (start us, length us, event | category | flops | bytes accessed | tf_op | source)
XLA Modules:
  0.0 12.7 jit_solution(16592094934593335679)
XLA Ops:
  0.0 12.1 %dirac_twice.1 = bf16[72,8,128]{2,1,0:T(8,128)(2,1)S(1)} custom-call(bf16[72,8,128]{2,1,0:T(8,128)(2,1)} %bitcast.16, bf16[36,4,128]{2,1,0:T(4,128)(2,1)} %bitcast.17), custom_call_target="tpu_custom_call" | custom-call | tf_op jit(solution)/shard_map/dirac_twice/pallas_call | solution.py:418
  12.1 0.7 %copy.7 = bf16[1,1,2,4,3,12,256]{6,3,5,4,2,1,0:T(4,128)(2,1)} copy(bf16[1,1,2,4,3,12,256]{6,3,5,4,2,1,0:T(4,128)(2,1)S(1)} %bitcast.15) | data formatting | bytes 294912

commit v5 on v4

--- a/solution.py
+++ b/solution.py
@@ -166,20 +166,10 @@
         lax.fori_loop(0, groups, body, 0)
 
     def first_application(load_sem, stage_sem, ready):
-        def block_loads(g):
-            rows = groups * 4
-            return [
-                pltpu.make_async_copy(
-                    source_hbm.at[pl.ds(block * rows + 4 * g, 4)],
-                    source.at[pl.ds(block * rows + 4 * g, 4)],
-                    load_sem.at[g],
-                )
-                for block in range(6)
-            ]
-
         def source_group(g):
+            piece = pl.ds(4 * g, 4)
             return pltpu.make_async_copy(
-                source_hbm.at[pl.ds(0, 24)], source.at[pl.ds(0, 24)], load_sem.at[g]
+                source_hbm.at[:, piece], source.at[:, piece], load_sem.at[g]
             )
 
         far_gauge = pltpu.make_async_copy(
@@ -188,10 +178,10 @@
         near_gauge = pltpu.make_async_copy(
             gauge_hbm.at[pl.ds(0, 18)], gauge.at[pl.ds(0, 18)], load_sem.at[groups + 1]
         )
-        far_gauge.start()
         for g in range(groups):
-            for load in block_loads(g):
-                load.start()
+            source_group(g).start()
+            if g == 0:
+                far_gauge.start()
         near_gauge.start()
 
         barrier = pltpu.get_barrier_semaphore()
@@ -210,7 +200,6 @@
 
         first_t, last_t, first_z, last_z = ta == 0, ta == nt - 1, gz == 0, gz == nz - 1
         stands_back = (lax.rem(ta, 2) == 1) & (ta > 1) & ~last_t
-        even, odd = lax.rem(ta, 2) == 0, lax.rem(ta, 2) == 1
         met_below_t, met_above_t = (ta > 0) & (ta != nt // 2), last_t | (ta == nt // 2 - 1)
         met_below_z, met_above_z = ~first_z, last_z
         signal_when(~met_above_t, barrier, above_t)
@@ -294,15 +283,16 @@
                 for s in range(2):
                     start_halo(0, halo, 2 * g + s)
 
-        far_gauge.wait()
-        put_links(3, 2)
         for g in range(groups):
             source_group(g).wait()
             for block in range(6):
                 for p in range(4):
                     at = (block * groups + g) * 4 + p
-                    wide[8 * at : 8 * at + 8] = source[at].astype(jnp.float32)
+                    wide[8 * at : 8 * at + 8] = source[block, 4 * g + p].astype(jnp.float32)
             tiles = {(ri, s, c): wide[rows_of(ri, s, c, g)] for ri, s, c in COMPONENTS}
+            if g == 0:
+                far_gauge.wait()
+                put_links(3, 2)
             for halo in range(4):
                 for s in range(2):
                     put_halo(0, halo, 2 * g + s, s, lambda *k: tiles[k])
@@ -421,7 +411,7 @@
         in_specs=[pl.BlockSpec(memory_space=pltpu.HBM)] * 2,
         out_specs=pl.BlockSpec(memory_space=pltpu.VMEM),
         scratch_shapes=[
-            pltpu.VMEM(source_rows.shape, jnp.bfloat16),
+            pltpu.VMEM((6, rhs, 8, LANES), jnp.bfloat16),
             pltpu.VMEM(gauge_rows.shape, jnp.bfloat16),
             pltpu.VMEM((48 * rhs, LANES), jnp.float32),
             pltpu.VMEM((2, groups, 24, 8, LANES), jnp.float32),
@@ -434,7 +424,7 @@
         ],
         compiler_params=pltpu.CompilerParams(collective_id=0, has_side_effects=True),
         name="dirac_twice",
-    )(source_rows, gauge_rows)
+    )(source_rows.reshape(6, rhs, 8, LANES), gauge_rows)
     out = rows.reshape(2, 3, rhs, 2, 4, LANES).transpose(0, 4, 1, 2, 3, 5)
     return out.reshape(source.shape)
 

time: 12.9 us -> 12.8 us (level)
  no operation moved by 1% of the time
where the time goes in v5:
time: 12.8 us; the launch traced here: 12.6 us
  Pallas kernels  12 us (94%)
  local copies, waits for them, and re-layouts  0.66 us (5%)
    pallas_call x1, Pallas kernels, body(): pl.pallas_call(functools.partial(kernel, groups), out_shape=pltpu.VMEM(so...  12 us
    unnamed x1, local copies, waits for them, and re-layouts  0.66 us

profile of v5, /device:TPU:0, one launch (start us, length us, event | category | flops | bytes accessed | tf_op | source)
XLA Modules:
  0.0 12.6 jit_solution(5190939227527141114)
XLA Ops:
  0.0 12.0 %dirac_twice.1 = bf16[72,8,128]{2,1,0:T(8,128)(2,1)S(1)} custom-call(bf16[6,12,8,128]{3,2,1,0:T(8,128)(2,1)} %bitcast.16, bf16[36,4,128]{2,1,0:T(4,128)(2,1)} %bitcast.17), custom_call_target="tpu_custom_call" | custom-call | tf_op jit(solution)/shard_map/dirac_twice/pallas_call | solution.py:408
  12.0 0.7 %copy.7 = bf16[1,1,2,4,3,12,256]{6,3,5,4,2,1,0:T(4,128)(2,1)} copy(bf16[1,1,2,4,3,12,256]{6,3,5,4,2,1,0:T(4,128)(2,1)S(1)} %bitcast.15) | data formatting | bytes 294912

commit v6 on v5

--- a/solution.py
+++ b/solution.py
@@ -110,7 +110,7 @@
     return direction * 2 + (0 if hop_sign > 0 else 1)
 
 
-def kernel(
+def apply_twice(
     groups, source_hbm, gauge_hbm, out, source, gauge, wide, psi, acc, links, sent, got,
     send_sem, final_sem,
 ):
@@ -200,7 +200,8 @@
 
         first_t, last_t, first_z, last_z = ta == 0, ta == nt - 1, gz == 0, gz == nz - 1
         stands_back = (lax.rem(ta, 2) == 1) & (ta > 1) & ~last_t
-        met_below_t, met_above_t = (ta > 0) & (ta != nt // 2), last_t | (ta == nt // 2 - 1)
+        met_below_t = (ta > 0) & (ta != nt // 2) & ~last_t
+        met_above_t = last_t | (ta == nt // 2 - 1) | (ta == nt - 2)
         met_below_z, met_above_z = ~first_z, last_z
         signal_when(~met_above_t, barrier, above_t)
         signal_when(~met_below_t, barrier, below_t)
@@ -397,6 +398,14 @@
     landed(sent, final_sem.at[0]).wait_send()
 
 
+def kernel(groups, *refs):
+    pl.run_scoped(
+        functools.partial(apply_twice, groups, *refs),
+        pltpu.SemaphoreType.DMA((1,)),
+        pltpu.SemaphoreType.DMA((3,)),
+    )
+
+
 def body(source, gauge_field):
     rhs = source.shape[5]
     groups = rhs // 4
@@ -419,8 +428,6 @@
             pltpu.VMEM((8, 18, 8, LANES), jnp.float32),
             pltpu.VMEM((2, 4, chunks, 48, LANES), jnp.bfloat16),
             pltpu.VMEM((2, chunks, 4, 48, LANES), jnp.bfloat16),
-            pltpu.SemaphoreType.DMA((1,)),
-            pltpu.SemaphoreType.DMA((3,)),
         ],
         compiler_params=pltpu.CompilerParams(collective_id=0, has_side_effects=True),
         name="dirac_twice",

time: 12.8 us -> 12.8 us (level)
  no operation moved by 1% of the time
where the time goes in v6:
time: 12.8 us; the launch traced here: 12.6 us
  Pallas kernels  11.9 us (93%)
  local copies, waits for them, and re-layouts  0.66 us (5%)
    pallas_call x1, Pallas kernels, body(): pl.pallas_call(functools.partial(kernel, groups), out_shape=pltpu.VMEM(so...  11.9 us
    unnamed x1, local copies, waits for them, and re-layouts  0.66 us

profile of v6, /device:TPU:0, one launch (start us, length us, event | category | flops | bytes accessed | tf_op | source)
XLA Modules:
  0.0 12.6 jit_solution(7671771178211839378)
XLA Ops:
  0.0 11.9 %dirac_twice.1 = bf16[72,8,128]{2,1,0:T(8,128)(2,1)S(1)} custom-call(bf16[6,12,8,128]{3,2,1,0:T(8,128)(2,1)} %bitcast.16, bf16[36,4,128]{2,1,0:T(4,128)(2,1)} %bitcast.17), custom_call_target="tpu_custom_call" | custom-call | tf_op jit(solution)/shard_map/dirac_twice/pallas_call | solution.py:417
  11.9 0.7 %copy.7 = bf16[1,1,2,4,3,12,256]{6,3,5,4,2,1,0:T(4,128)(2,1)} copy(bf16[1,1,2,4,3,12,256]{6,3,5,4,2,1,0:T(4,128)(2,1)S(1)} %bitcast.15) | data formatting | bytes 294912

commit v7 on v6

--- a/solution.py
+++ b/solution.py
@@ -299,10 +299,10 @@
                     put_halo(0, halo, 2 * g + s, s, lambda *k: tiles[k])
             for k, tile in tiles.items():
                 psi[0, g, plane(*k)] = tile
+            start_when(met_below_t, 0, g)
+            start_when(met_above_t, 1, g)
             start_when(last_z & ~stands_back, 3, g)
             start_when(met_below_z & ~last_z, 2, g)
-            start_when(met_below_t, 0, g)
-            start_when(met_above_t, 1, g)
         start_all((last_z, 2))
         wait_for(ready.at[1], ~met_above_z)
         start_all((~met_above_z, 3))

time: 12.8 us -> 12.8 us (level)
  no operation moved by 1% of the time
where the time goes in v7:
time: 12.8 us; the launch traced here: 12.6 us
  Pallas kernels  11.9 us (93%)
  local copies, waits for them, and re-layouts  0.66 us (5%)
    pallas_call x1, Pallas kernels, body(): pl.pallas_call(functools.partial(kernel, groups), out_shape=pltpu.VMEM(so...  11.9 us
    unnamed x1, local copies, waits for them, and re-layouts  0.66 us

profile of v7, /device:TPU:0, one launch (start us, length us, event | category | flops | bytes accessed | tf_op | source)
XLA Modules:
  0.0 12.6 jit_solution(14605955023793823587)
XLA Ops:
  0.0 11.9 %dirac_twice.1 = bf16[72,8,128]{2,1,0:T(8,128)(2,1)S(1)} custom-call(bf16[6,12,8,128]{3,2,1,0:T(8,128)(2,1)} %bitcast.16, bf16[36,4,128]{2,1,0:T(4,128)(2,1)} %bitcast.17), custom_call_target="tpu_custom_call" | custom-call | tf_op jit(solution)/shard_map/dirac_twice/pallas_call | solution.py:417
  11.9 0.7 %copy.7 = bf16[1,1,2,4,3,12,256]{6,3,5,4,2,1,0:T(4,128)(2,1)} copy(bf16[1,1,2,4,3,12,256]{6,3,5,4,2,1,0:T(4,128)(2,1)S(1)} %bitcast.15) | data formatting | bytes 294912

commit v8 on v7

--- a/solution.py
+++ b/solution.py
@@ -352,8 +352,14 @@
                             )
                     for halo in (0, 1, far):
                         put_halo(1, halo, q, s, lambda *k: total[k])
-                    for halo in (0, 1, far):
-                        start_halo(1, halo, q)
+                    start_halo(1, 0, q)
+                    start_halo(1, 1, q)
+                    if far == 2:
+                        @pl.when(~held)
+                        def _():
+                            start_halo(1, far, q)
+                    else:
+                        start_halo(1, far, q)
                     for k, tile in total.items():
                         psi[1, g, plane(*k)] = tile
                 return carry
@@ -370,6 +376,9 @@
         @pl.when(upper == 1)
         def _():
             stages(3, 2)
+
+        plane_hops(1)
+        start_all((held, 2), step=1)
 
     pl.run_scoped(
         first_application,
@@ -377,7 +386,6 @@
         pltpu.SemaphoreType.DMA((2, chunks)),
         pltpu.SemaphoreType.REGULAR((3,)),
     )
-    plane_hops(1)
 
     for g in range(groups):
         for s in range(2):

time: 12.8 us -> 12.8 us (level)
  no operation moved by 1% of the time
where the time goes in v8:
time: 12.8 us; the launch traced here: 12.6 us
  Pallas kernels  11.9 us (93%)
  local copies, waits for them, and re-layouts  0.66 us (5%)
    pallas_call x1, Pallas kernels, body(): pl.pallas_call(functools.partial(kernel, groups), out_shape=pltpu.VMEM(so...  11.9 us
    unnamed x1, local copies, waits for them, and re-layouts  0.66 us

profile of v8, /device:TPU:0, one launch (start us, length us, event | category | flops | bytes accessed | tf_op | source)
XLA Modules:
  0.0 12.6 jit_solution(5996296977756962265)
XLA Ops:
  0.0 11.9 %dirac_twice.1 = bf16[72,8,128]{2,1,0:T(8,128)(2,1)S(1)} custom-call(bf16[6,12,8,128]{3,2,1,0:T(8,128)(2,1)} %bitcast.16, bf16[36,4,128]{2,1,0:T(4,128)(2,1)} %bitcast.17), custom_call_target="tpu_custom_call" | custom-call | tf_op jit(solution)/shard_map/dirac_twice/pallas_call | solution.py:425
  11.9 0.7 %copy.7 = bf16[1,1,2,4,3,12,256]{6,3,5,4,2,1,0:T(4,128)(2,1)} copy(bf16[1,1,2,4,3,12,256]{6,3,5,4,2,1,0:T(4,128)(2,1)S(1)} %bitcast.15) | data formatting | bytes 294912
